TPU v7x, 32 devices: a whole 2x2x4 slice. The times are simulated.
32 devices in a mesh: gx: 4 (over z), gy: 4 (over y, core), gz: 2 (over x).
Axes of the slice: x: 2, y: 2, z: 4, core: 2. Of those that a mesh axis runs over, the one named last changes fastest.
Arguments:
- gradients: bfloat16 [32, 768, 512], P(('gx', 'gy', 'gz')), may hold values from -6 to 6
- master_weights: float32 [768, 512], P(('gx', 'gy', 'gz')), may hold values from -10 to 10
- first_moment: float32 [768, 512], P(('gx', 'gy', 'gz')), may hold values from -8 to 8
- second_moment: float32 [768, 512], P(('gx', 'gy', 'gz')), may hold values from 1 to 100
- tensor_ids: int32 [768], P(('gx', 'gy', 'gz')), may hold values from 0 to 3, as said below
Outputs:
- new_master: float32 [768, 512], P(('gx', 'gy', 'gz'))
- new_first: float32 [768, 512], P(('gx', 'gy', 'gz'))
- new_second: float32 [768, 512], P(('gx', 'gy', 'gz'))
- scaled_update: float32 [768, 512], P(('gx', 'gy', 'gz'))
- params: bfloat16 [768, 512], replicated
Inputs may be any that keep to these rules, and one draw needn't show every extreme that they name: `tensor_ids`: nondecreasing along the rows; every tensor of 4 owns one contiguous run of rows.
All inputs are finite; a program needn't handle non-finite values.
Results may differ from a plain program's by a relative error of at most 0.0045.
Values may be sent and summed in bfloat16 or wider, within the bound.
A program may use at most 64 MiB of HBM per device.

v0:
```python
import jax
import jax.numpy as jnp
from jax import lax
from jax.sharding import PartitionSpec as P

NT = 4
decay_first = 0.9
decay_second = 0.999
epsilon = 1e-06
weight_decay = 0.01
step_size = 0.05


def tensor_sums(values, onehot):
    return jnp.dot(jnp.sum(values * values, axis=1), onehot, precision=lax.Precision.HIGHEST)


def on_device(gradients, master_weights, first_moment, second_moment, tensor_ids):
    count_across = lax.axis_size("gx")
    count_down = lax.axis_size("gy")
    count_along = lax.axis_size("gz")
    own_rows, row_width = master_weights.shape
    own_gradient = gradients[0].astype(jnp.float32)
    onehot = (tensor_ids[:, None] == jnp.arange(NT, dtype=jnp.int32)[None, :]).astype(jnp.float32)
    counts = jnp.sum(onehot, axis=0) * row_width
    weight_local = tensor_sums(master_weights, onehot)
    summed = lax.psum_scatter(own_gradient, ("gx", "gy", "gz"), scatter_dimension=0, tiled=True)
    new_first = decay_first * first_moment + (1.0 - decay_first) * summed
    new_second = decay_second * second_moment + (1.0 - decay_second) * summed * summed
    update = new_first / (jnp.sqrt(new_second) + epsilon) + weight_decay * master_weights
    update_local = tensor_sums(update, onehot)
    weight_sq, update_sq, total_counts = lax.psum(
        (weight_local, update_local, counts), ("gx", "gy", "gz")
    )
    trust_ratio = jnp.sqrt(weight_sq / (update_sq + total_counts))
    row_trust = jnp.dot(onehot, trust_ratio, precision=lax.Precision.HIGHEST)
    scaled_update = row_trust[:, None] * update
    new_master = master_weights - step_size * scaled_update
    params = new_master.astype(jnp.bfloat16)
    stacked = params.reshape(1, 1, 1, own_rows, row_width)
    stacked = lax.all_gather(stacked, "gz", axis=2, tiled=True)
    stacked = lax.all_gather(stacked, "gy", axis=1, tiled=True)
    stacked = lax.all_gather(stacked, "gx", axis=0, tiled=True)
    gathered = stacked.reshape(count_across * count_down * count_along * own_rows, row_width)
    return (new_master, new_first, new_second, scaled_update, gathered)


def solution(mesh):
    placed = (
        P(("gx", "gy", "gz"), None, None),
        P(("gx", "gy", "gz"), None),
        P(("gx", "gy", "gz"), None),
        P(("gx", "gy", "gz"), None),
        P(("gx", "gy", "gz")),
    )
    return jax.shard_map(
        on_device,
        mesh=mesh,
        in_specs=placed,
        out_specs=(
            P(("gx", "gy", "gz"), None),
            P(("gx", "gy", "gz"), None),
            P(("gx", "gy", "gz"), None),
            P(("gx", "gy", "gz"), None),
            P(),
        ),
        check_vma=False,
    )
```

profile of v0, /device:TPU:0, one launch (start us, length us, event | category | flops | bytes accessed | tf_op | source)
XLA Modules:
  0.0 192.9 jit_solution(224679185084797779)
XLA Ops:
  7.2 0.0 copy-start.3
  7.2 0.0 copy-start
  7.2 0.0 copy-start.1
  7.2 0.0 copy-start.2
  7.2 0.0 reduce-scatter.2.cloned.1.call-start
  7.3 2.5 %bitcast_convert_fusion = f32[768,512]{1,0:T(8,128)} fusion(bf16[1,768,512]{2,1,0:T(8,128)(2,1)} %param.5), kind=kLoop, calls=%fused_computation.4 | loop fusion | flops 393216 | bytes 2359296 | tf_op jit(solution)/shard_map/convert_element_type | solution.py:23
  9.8 0.0 reduce-scatter.2.cloned.1.call-update
  9.8 0.0 copy-done.3
  9.8 0.1 convert_reduce_fusion
  9.9 104.0 %reduce-scatter.2.cloned.1.call-done = f32[24,512]{1,0:T(8,128)} async-done(((f32[768,512]{1,0:T(8,128)}), f32[24,512]{1,0:T(8,128)}) %reduce-scatter.2.cloned.1.call-update) | async-done | bytes 49168 | tf_op jit(solution)/shard_map/reduce_scatter | solution.py:27
  113.9 0.0 copy-done
  113.9 0.0 copy-done.1
  113.9 0.0 copy-done.2
  113.9 1.6 multiply_reduce_fusion
  115.5 0.1 fusion
  115.6 0.1 convolution_bitcast_fusion.2
  115.7 40.1 %all-reduce = (f32[4]{0:T(128)S(1)}, f32[4]{0:T(128)S(1)}) all-reduce(f32[4]{0:T(128)S(1)} %convolution_bitcast_fusion.2, f32[4]{0:T(128)S(1)} %fusion), channel_id=1, replica_groups=mesh['gx'=4,'gy'=4,'gz'=2] {'gx','gy','gz'}, use_global_device_ids=true, to_apply=%region_1.0 | all-reduce | flops 8 | bytes 64 | tf_op jit(solution)/shard_map/psum | solution.py:32
  155.8 0.1 convolution_bitcast_fusion
  155.9 0.7 fusion.8
  156.6 4.7 %all-gather = bf16[48,512]{1,0:T(8,128)(2,1)S(1)} all-gather(bf16[24,512]{1,0:T(8,128)(2,1)S(1)} %get-tuple-element.7), channel_id=2, replica_groups=mesh['gx'=4,'gy'=4,'gz'=2] {'gz'}, dimensions={0}, use_global_device_ids=true | all-gather | bytes 73728 | tf_op jit(solution)/shard_map/all_gather | solution.py:41
  161.4 5.9 %all_gather.10 = bf16[1,4,2,24,512]{4,3,2,0,1:T(8,128)(2,1)S(1)} all-gather(bf16[1,1,2,24,512]{4,3,2,0,1:T(8,128)(2,1)S(1)} %bitcast.25), channel_id=1, replica_groups=mesh['gx'=4,'gy'=4,'gz'=2] {'gy'}, dimensions={1}, use_global_device_ids=true | all-gather | bytes 245760 | tf_op jit(solution)/shard_map/all_gather | solution.py:42
  167.3 17.9 %all_gather.11 = bf16[4,4,2,24,512]{4,3,2,1,0:T(8,128)(2,1)S(1)} all-gather(bf16[1,4,2,24,512]{4,3,2,1,0:T(8,128)(2,1)S(1)} %bitcast.24), channel_id=1, replica_groups=mesh['gx'=4,'gy'=4,'gz'=2] {'gx'}, dimensions={0}, use_global_device_ids=true | all-gather | bytes 983040 | tf_op jit(solution)/shard_map/all_gather | solution.py:43
  185.2 0.9 copy.13
Async XLA Ops:
  7.2 2.6 %copy-start.3 = (s32[24]{0:T(128)S(1)}, s32[24]{0:T(128)}, u32[]{:S(2)}) copy-start(s32[24]{0:T(128)} %param.9) | copy-start | bytes 292
  7.2 106.7 %copy-start = (f32[24,512]{1,0:T(8,128)S(1)}, f32[24,512]{1,0:T(8,128)}, u32[]{:S(2)}) copy-start(f32[24,512]{1,0:T(8,128)} %param.6) | copy-start | bytes 147460
  7.2 106.7 %copy-start.1 = (f32[24,512]{1,0:T(8,128)S(1)}, f32[24,512]{1,0:T(8,128)}, u32[]{:S(2)}) copy-start(f32[24,512]{1,0:T(8,128)} %param.8) | copy-start | bytes 147460
  7.2 106.7 %copy-start.2 = (f32[24,512]{1,0:T(8,128)S(1)}, f32[24,512]{1,0:T(8,128)}, u32[]{:S(2)}) copy-start(f32[24,512]{1,0:T(8,128)} %param.7) | copy-start | bytes 147460
  7.2 106.7 %reduce-scatter.2.cloned.1.call-start = ((), (), s32[]{:S(2)}) async-start(), calls=%async_computation.1 | async-start | bytes 1622016 | tf_op jit(solution)/shard_map/reduce_scatter | solution.py:27
Sparse Core Ops, SparseCore 0:
  13.3 100.5 reduce-scatter.1
where the time goes:
time: 193 us
  waiting for transfers between devices  104 us (54%)
  blocking collectives  68.6 us (36%)
  between operations  14.1 us (7%)
  other arithmetic  4.92 us (3%)
    reduce_scatter x1, waiting for transfers between devices, on_device(): lax.psum_scatter(own_gradient, ('gx', 'gy', 'gz'), scatter_dimension=0, t...  104 us
    psum x1, blocking collectives, on_device(): lax.psum((weight_local, update_local, counts), ('gx', 'gy', 'gz'))  40.1 us
    all_gather x1, blocking collectives, on_device(): stacked = lax.all_gather(stacked, 'gx', axis=0, tiled=True)  17.9 us
    all_gather x1, blocking collectives, on_device(): stacked = lax.all_gather(stacked, 'gy', axis=1, tiled=True)  5.92 us
    all_gather x1, blocking collectives, on_device(): stacked = lax.all_gather(stacked, 'gz', axis=2, tiled=True)  4.72 us
  transfers between devices with their start and end apart: 1, of which 1 were waited for; matrix products, arithmetic and copies ran while one was open for 0% of the time, Pallas kernels for 0%

commit v1 on v0

--- a/solution.py
+++ b/solution.py
@@ -30,7 +30,7 @@
     update = new_first / (jnp.sqrt(new_second) + epsilon) + weight_decay * master_weights
     update_local = tensor_sums(update, onehot)
     weight_sq, update_sq, total_counts = lax.psum(
-        (weight_local, update_local, counts), ("gx", "gy", "gz")
+        lax.psum((weight_local, update_local, counts), axis_name=("gy", "gz")), axis_name="gx"
     )
     trust_ratio = jnp.sqrt(weight_sq / (update_sq + total_counts))
     row_trust = jnp.dot(onehot, trust_ratio, precision=lax.Precision.HIGHEST)

time: 193 us -> 176 us (0.912)
  blocking collectives: 68.6 us -> 51.9 us
    psum x1 -> x2, blocking collectives: 40.1 us -> 24.1 us  [the longest x1 13.4 us: on_device(): lax.psum((weight_local, update_local, counts), axis_name=('gy', 'gz'))]
where the time goes in v1:
time: 176 us
  waiting for transfers between devices  104 us (59%)
  blocking collectives  51.9 us (29%)
  between operations  14.1 us (8%)
  other arithmetic  4.92 us (3%)
    reduce_scatter x1, waiting for transfers between devices, on_device(): lax.psum_scatter(own_gradient, ('gx', 'gy', 'gz'), scatter_dimension=0, t...  104 us
    all_gather x1, blocking collectives, on_device(): stacked = lax.all_gather(stacked, 'gx', axis=0, tiled=True)  17.7 us
    psum x1, blocking collectives, on_device(): lax.psum((weight_local, update_local, counts), axis_name=('gy', 'gz'))  13.4 us
    psum x1, blocking collectives, on_device(): lax.psum(lax.psum((weight_local, update_local, counts), axis_name=('gy',...  10.7 us
    all_gather x1, blocking collectives, on_device(): stacked = lax.all_gather(stacked, 'gy', axis=1, tiled=True)  5.58 us
    all_gather x1, blocking collectives, on_device(): stacked = lax.all_gather(stacked, 'gz', axis=2, tiled=True)  4.48 us
  transfers between devices with their start and end apart: 1, of which 1 were waited for; matrix products, arithmetic and copies ran while one was open for 0% of the time, Pallas kernels for 0%

profile of v1, /device:TPU:0, one launch (start us, length us, event | category | flops | bytes accessed | tf_op | source)
XLA Modules:
  0.0 176.2 jit_solution(2148480315237815568)
XLA Ops:
  7.2 0.0 copy-start.3
  7.2 0.0 copy-start
  7.2 0.0 copy-start.1
  7.2 0.0 copy-start.2
  7.2 0.0 reduce-scatter.2.cloned.1.call-start
  7.3 2.5 %bitcast_convert_fusion = f32[768,512]{1,0:T(8,128)} fusion(bf16[1,768,512]{2,1,0:T(8,128)(2,1)} %param.5), kind=kLoop, calls=%fused_computation.4 | loop fusion | flops 393216 | bytes 2359296 | tf_op jit(solution)/shard_map/convert_element_type | solution.py:23
  9.8 0.0 reduce-scatter.2.cloned.1.call-update
  9.8 0.0 copy-done.3
  9.8 0.1 convert_reduce_fusion
  9.9 104.0 %reduce-scatter.2.cloned.1.call-done = f32[24,512]{1,0:T(8,128)} async-done(((f32[768,512]{1,0:T(8,128)}), f32[24,512]{1,0:T(8,128)}) %reduce-scatter.2.cloned.1.call-update) | async-done | bytes 49168 | tf_op jit(solution)/shard_map/reduce_scatter | solution.py:27
  113.9 0.0 copy-done
  113.9 0.0 copy-done.1
  113.9 0.0 copy-done.2
  113.9 1.6 multiply_reduce_fusion
  115.5 0.1 fusion
  115.6 0.1 convolution_bitcast_fusion.2
  115.7 13.4 %all-reduce = (f32[4]{0:T(128)S(1)}, f32[4]{0:T(128)S(1)}) all-reduce(f32[4]{0:T(128)S(1)} %convolution_bitcast_fusion.2, f32[4]{0:T(128)S(1)} %fusion), channel_id=1, replica_groups=mesh['gx'=4,'gy'=4,'gz'=2] {'gy','gz'}, use_global_device_ids=true, to_apply=%region_1.0 | all-reduce | flops 8 | bytes 64 | tf_op jit(solution)/shard_map/psum | solution.py:33
  129.1 10.7 %all-reduce.1 = (f32[4]{0:T(128)S(1)}, f32[4]{0:T(128)S(1)}) all-reduce(f32[4]{0:T(128)S(1)} %get-tuple-element.5, f32[4]{0:T(128)S(1)} %get-tuple-element.6), channel_id=1, replica_groups=mesh['gx'=4,'gy'=4,'gz'=2] {'gx'}, use_global_device_ids=true, to_apply=%region_2.0 | all-reduce | flops 8 | bytes 64 | tf_op jit(solution)/shard_map/psum | solution.py:32
  139.8 0.1 convolution_bitcast_fusion
  139.9 0.7 fusion.8
  140.7 4.5 %all-gather = bf16[48,512]{1,0:T(8,128)(2,1)S(1)} all-gather(bf16[24,512]{1,0:T(8,128)(2,1)S(1)} %get-tuple-element.9), channel_id=2, replica_groups=mesh['gx'=4,'gy'=4,'gz'=2] {'gz'}, dimensions={0}, use_global_device_ids=true | all-gather | bytes 73728 | tf_op jit(solution)/shard_map/all_gather | solution.py:41
  145.1 5.6 %all_gather.10 = bf16[1,4,2,24,512]{4,3,2,0,1:T(8,128)(2,1)S(1)} all-gather(bf16[1,1,2,24,512]{4,3,2,0,1:T(8,128)(2,1)S(1)} %bitcast.25), channel_id=1, replica_groups=mesh['gx'=4,'gy'=4,'gz'=2] {'gy'}, dimensions={1}, use_global_device_ids=true | all-gather | bytes 245760 | tf_op jit(solution)/shard_map/all_gather | solution.py:42
  150.7 17.7 %all_gather.11 = bf16[4,4,2,24,512]{4,3,2,1,0:T(8,128)(2,1)S(1)} all-gather(bf16[1,4,2,24,512]{4,3,2,1,0:T(8,128)(2,1)S(1)} %bitcast.24), channel_id=1, replica_groups=mesh['gx'=4,'gy'=4,'gz'=2] {'gx'}, dimensions={0}, use_global_device_ids=true | all-gather | bytes 983040 | tf_op jit(solution)/shard_map/all_gather | solution.py:43
  168.5 0.9 copy.13
Async XLA Ops:
  7.2 2.6 %copy-start.3 = (s32[24]{0:T(128)S(1)}, s32[24]{0:T(128)}, u32[]{:S(2)}) copy-start(s32[24]{0:T(128)} %param.9) | copy-start | bytes 292
  7.2 106.7 %copy-start = (f32[24,512]{1,0:T(8,128)S(1)}, f32[24,512]{1,0:T(8,128)}, u32[]{:S(2)}) copy-start(f32[24,512]{1,0:T(8,128)} %param.6) | copy-start | bytes 147460
  7.2 106.7 %copy-start.1 = (f32[24,512]{1,0:T(8,128)S(1)}, f32[24,512]{1,0:T(8,128)}, u32[]{:S(2)}) copy-start(f32[24,512]{1,0:T(8,128)} %param.8) | copy-start | bytes 147460
  7.2 106.7 %copy-start.2 = (f32[24,512]{1,0:T(8,128)S(1)}, f32[24,512]{1,0:T(8,128)}, u32[]{:S(2)}) copy-start(f32[24,512]{1,0:T(8,128)} %param.7) | copy-start | bytes 147460
  7.2 106.7 %reduce-scatter.2.cloned.1.call-start = ((), (), s32[]{:S(2)}) async-start(), calls=%async_computation.1 | async-start | bytes 1622016 | tf_op jit(solution)/shard_map/reduce_scatter | solution.py:27
Sparse Core Ops, SparseCore 0:
  13.3 100.5 reduce-scatter.1
